TPU v7x, 32 devices: a whole 2x2x4 slice. The times are simulated.
32 devices in a mesh: sky: 2 (over y), ma: 4 (over z), freq: 2 (over x), pol: 2 (over core).
Axes of the slice: x: 2, y: 2, z: 4, core: 2. Of those that a mesh axis runs over, the one named last changes fastest.
Arguments:
- alm: bfloat16 [2, 2, 1024, 4, 1024], P(None, 'freq', ('ma', 'pol'), None, 'sky'), parts along dimension 4, may hold values from -6 to 6
- beam: bfloat16 [4, 2, 2, 1024, 1024], P('ma', 'freq', None, 'pol'), may hold values from -0.1875 to 0.1875
- m_table: int32 [4], P('ma'), may hold values from 0 to 511, as said below
- chan_mask: int32 [2], P('freq'), may hold values from 0 to 1, as said below
- noise: float32 [2, 1024], P('freq', 'pol'), may hold values from 0.5 to 4
Outputs:
- scaled: bfloat16 [2, 2, 4, 1024, 1024], P(None, 'freq', 'ma', 'pol', 'sky'), parts along dimension 4
- channel_power: float32 [4], P(('sky', 'freq')), parts along dimension 0
There are 2 independent parts, one for each index of `sky`. A program takes and returns all parts, laid end to end along the dimension named above; an argument that names none is the same for every part. Nothing has to cross between parts.
Inputs may be any that keep to these rules, and one draw needn't show every extreme that they name: `m_table`: the 4 values are distinct whole numbers below 512. `chan_mask`: at least one of the 2 channels is usable.
All inputs are finite; a program needn't handle non-finite values.
Results may differ from a plain program's by a relative error of at most 0.00055.
Values may be sent and summed in bfloat16 or wider, within the bound.
A program may use at most 64 MiB of HBM per device.

v0:
```python
import jax
import jax.numpy as jnp
from jax import lax
from jax.sharding import PartitionSpec as P


def on_device(alm, beam, m_table, chan_mask, noise):
    arrived = lax.all_to_all(alm, "ma", split_axis=3, concat_axis=2, tiled=True)
    blocks = arrived.reshape(
        arrived.shape[0],
        arrived.shape[1],
        lax.axis_size("ma"),
        arrived.shape[2] // lax.axis_size("ma"),
        arrived.shape[4],
    )
    joined = lax.all_gather(blocks, "pol", axis=3, tiled=True)
    coeffs_all = joined.reshape(
        joined.shape[0], joined.shape[1], joined.shape[2] * joined.shape[3], joined.shape[4]
    )
    degree = lax.iota(jnp.int32, coeffs_all.shape[2])
    keep_mask = (degree >= m_table[0])[None, None, :, None]
    coeffs = jnp.where(keep_mask, coeffs_all, jnp.zeros((), coeffs_all.dtype))
    response = beam[0]
    real_part = jnp.einsum(
        "fkl,fls->fks", response[:, 0], coeffs[0], preferred_element_type=jnp.float32
    ) - jnp.einsum("fkl,fls->fks", response[:, 1], coeffs[1], preferred_element_type=jnp.float32)
    imag_part = jnp.einsum(
        "fkl,fls->fks", response[:, 0], coeffs[1], preferred_element_type=jnp.float32
    ) + jnp.einsum("fkl,fls->fks", response[:, 1], coeffs[0], preferred_element_type=jnp.float32)
    visibility = jnp.stack([real_part, imag_part])
    weighted = visibility * visibility / noise[None, :, :, None]
    partial_power = jnp.sum(weighted, axis=(0, 2, 3))
    modes_total = jnp.float32(
        lax.axis_size("ma") * noise.shape[1] * lax.axis_size("pol") * visibility.shape[3]
    )
    mask_float = chan_mask.astype(jnp.float32)
    channel_power = lax.psum(partial_power, ("ma", "pol")) / modes_total
    masked_sum, live_count = lax.psum(
        (jnp.sum(mask_float * channel_power), jnp.sum(mask_float)), "freq"
    )
    band_power = masked_sum / live_count
    factor = mask_float / jnp.sqrt(0.5 * channel_power + 0.5 * band_power + 1e-06)
    scaled = visibility * (lax.rsqrt(noise) * factor[:, None])[None, :, :, None]
    return (scaled[:, :, None].astype(jnp.bfloat16), channel_power)


def solution(mesh):
    return jax.shard_map(
        on_device,
        mesh=mesh,
        in_specs=(
            P(None, "freq", ("ma", "pol"), None, "sky"),
            P("ma", "freq", None, "pol", None),
            P("ma"),
            P("freq"),
            P("freq", "pol"),
        ),
        out_specs=(P(None, "freq", "ma", "pol", "sky"), P(("sky", "freq"))),
        check_vma=False,
    )
```

profile of v0, /device:TPU:0, one launch (start us, length us, event | category | flops | bytes accessed | tf_op | source)
XLA Modules:
  0.0 94.6 jit_solution(7890521315917420241)
XLA Ops:
  7.2 0.0 all-gather.3.cloned.1.call-start
  7.2 1.4 %copy.10 = bf16[2,1,128,4,512]{4,2,0,1,3:T(8,128)(2,1)S(1)} copy(bf16[2,1,128,4,512]{4,3,2,1,0:T(4,128)(2,1)} %param.5) | data formatting | bytes 2097152 | tf_op args[0]
  8.6 31.9 %all_to_all.15 = bf16[2,1,128,4,512]{4,2,0,1,3:T(8,128)(2,1)S(1)} all-to-all(bf16[2,1,128,4,512]{4,2,0,1,3:T(8,128)(2,1)S(1)} %copy.10), channel_id=1, replica_groups=mesh['sky'=2,'ma'=4,'freq'=2,'pol'=2] {'ma'}, dimensions={3} | all-to-all | bytes 2097152 | tf_op jit(solution)/shard_map/all_to_all | solution.py:8
  40.5 1.1 %copy.14 = bf16[2,1,128,4,512]{4,2,3,0,1:T(8,128)(2,1)} copy(bf16[2,1,128,4,512]{4,2,0,1,3:T(8,128)(2,1)S(1)} %all_to_all.15) | data formatting | bytes 2097152 | tf_op jit(solution)/shard_map/all_to_all | solution.py:8
  41.6 0.0 all-gather.3.cloned.1.call-update
  42.9 8.5 %all-gather.3.cloned.1.call-done = bf16[2,1,4,256,1,512]{5,3,2,0,4,1:T(8,128)(2,1)} async-done(((bf16[2,1,4,128,1,512]{5,3,2,0,4,1:T(8,128)(2,1)}), bf16[2,1,4,256,1,512]{5,3,2,0,4,1:T(8,128)(2,1)}) %all-gather.3.cloned.1.call-update) | async-done | bytes 2097168 | tf_op jit(solution)/shard_map/all_gather | solution.py:16
  51.5 0.0 copy-start.1
  51.5 2.0 %broadcast_select_fusion = bf16[2,1,1024,512]{3,2,0,1:T(8,128)(2,1)S(1)} fusion(bf16[2,1,1024,512]{3,2,0,1:T(8,128)(2,1)} %bitcast.47, pred[1024]{0:T(1024)(128)(4,1)S(1)} %iota_compare_fusion), kind=kLoop, calls=%fused_computation.5 | loop fusion | flops 1048576 | bytes 4195328 | tf_op jit(solution)/shard_map/jit(_where)/select_n | solution.py:22
  53.4 0.3 copy-done.1
  53.7 0.7 fusion.3
  54.4 0.8 fusion.4
  55.2 0.8 convolution_subtract_fusion
  55.9 0.0 copy-start
  56.0 0.8 convolution_add_fusion
  56.7 0.0 copy-done
  56.7 1.1 %fusion.2 = f32[]{:T(128)} fusion(f32[1,1,512,512]{2,3,1,0:T(8,128)S(1)} %bitcast.45, f32[1,1,512,512]{2,3,1,0:T(8,128)S(1)} %bitcast.43, f32[512]{0:T(512)S(1)} %bitcast.48), kind=kLoop, calls=%fused_computation.4 | loop fusion | flops 2097151 | bytes 2099204 | tf_op jit(solution)/shard_map/reduce_sum | solution.py:32
  57.9 17.7 %psum.21 = f32[1]{0:T(128)} all-reduce(f32[1]{0:T(128)} %bitcast.16), channel_id=1, replica_groups=mesh['sky'=2,'ma'=4,'freq'=2,'pol'=2] {'ma','pol'}, use_global_device_ids=true, to_apply=%region_1.2 | all-reduce | flops 1 | bytes 8 | tf_op jit(solution)/shard_map/psum | solution.py:37
  76.9 6.7 %all-reduce = (f32[]{:T(128)}, f32[]{:T(128)}) all-reduce(f32[]{:T(128)} %bitcast.17, f32[]{:T(128)} %bitcast.18), channel_id=1, replica_groups=mesh['sky'=2,'ma'=4,'freq'=2,'pol'=2] {'freq'}, use_global_device_ids=true, to_apply=%region_2.3 | all-reduce | flops 2 | bytes 16 | tf_op jit(solution)/shard_map/psum | solution.py:38
  85.0 0.3 fusion
  85.3 1.3 %copy.12 = bf16[2,1,1,512,512]{4,3,2,1,0:T(8,128)(2,1)} copy(bf16[2,1,1,512,512]{3,4,2,1,0:T(8,128)(2,1)S(1)} %fusion) | data formatting | bytes 2097152
  (2 shorter events, 0.0 us)
Async XLA Ops:
  7.2 44.3 %all-gather.3.cloned.1.call-start = ((), (), s32[]{:S(2)}) async-start(), calls=%async_computation.1 | async-start | bytes 3145728 | tf_op jit(solution)/shard_map/all_gather | solution.py:16
  51.5 2.2 %copy-start.1 = (bf16[1,1,2,512,1024]{4,3,2,1,0:T(8,128)(2,1)S(1)}, bf16[1,1,2,512,1024]{4,3,2,1,0:T(8,128)(2,1)}, u32[]{:S(2)}) copy-start(bf16[1,1,2,512,1024]{4,3,2,1,0:T(8,128)(2,1)} %param.6) | copy-start | bytes 6291460
  55.9 0.8 copy-start
Sparse Core Ops, SparseCore 0:
  41.7 9.6 all-gather.2
where the time goes:
time: 94.9 us; the launch traced here: 94.6 us
  blocking collectives  56.3 us (59%)
  between operations  19.3 us (20%)
  waiting for transfers between devices  8.54 us (9%)
  local copies, waits for them, and re-layouts  4.09 us (4%)
  other arithmetic  3.39 us (4%)
  matrix products  3.01 us (3%)
    all_to_all x1, blocking collectives, on_device(): arrived = lax.all_to_all(alm, 'ma', split_axis=3, concat_axis=2, tiled=True)  31.9 us
    psum x1, blocking collectives, on_device(): channel_power = lax.psum(partial_power, ('ma', 'pol')) / modes_total  17.7 us
    all_gather x1, waiting for transfers between devices, on_device(): joined = lax.all_gather(blocks, 'pol', axis=3, tiled=True)  8.53 us
    psum x1, blocking collectives, on_device(): lax.psum((jnp.sum(mask_float * channel_power), jnp.sum(mask_float)), 'freq')  6.71 us
    unnamed x6, local copies, waits for them, and re-layouts  3.01 us
    select_n x1, other arithmetic, on_device(): coeffs = jnp.where(keep_mask, coeffs_all, jnp.zeros((), coeffs_all.dtype))  1.96 us
  transfers between devices with their start and end apart: 1, of which 1 were waited for; matrix products, arithmetic and copies ran while one was open for 0% of the time, Pallas kernels for 0%

commit v1 on v0

--- a/solution.py
+++ b/solution.py
@@ -4,8 +4,19 @@
 from jax.sharding import PartitionSpec as P
 
 
+def loops_follow(m):
+    q_next = lax.all_to_all(
+        jnp.stack(jnp.split(m, lax.psum(1, axis_name="ma"), axis=3)),
+        axis_name="ma",
+        split_axis=0,
+        concat_axis=0,
+    )
+    h_now = jnp.concatenate(q_next, axis=2)
+    return h_now
+
+
 def on_device(alm, beam, m_table, chan_mask, noise):
-    arrived = lax.all_to_all(alm, "ma", split_axis=3, concat_axis=2, tiled=True)
+    arrived = loops_follow(alm)
     blocks = arrived.reshape(
         arrived.shape[0],
         arrived.shape[1],

time: 94.9 us -> 98.4 us (1.037)
  local copies, waits for them, and re-layouts: 4.09 us -> 9.32 us
  other arithmetic: 3.39 us -> 1.79 us
    split x0 -> x1, local copies, waits for them, and re-layouts: none -> 4.66 us  [loops_follow(): jnp.split(m, lax.psum(1, axis_name='ma'), axis=3)]
    select_n x1, other arithmetic: 1.96 us -> 0.22 us  [on_device(): coeffs = jnp.where(keep_mask, coeffs_all, jnp.zeros((), coeffs_all.dtype))]
    all_gather x0 -> x1, local copies, waits for them, and re-layouts: none -> 1.73 us  [on_device(): joined = lax.all_gather(blocks, 'pol', axis=3, tiled=True)]
    all_to_all x1 -> x0, local copies, waits for them, and re-layouts: 1.08 us -> none  [on_device(): arrived = lax.all_to_all(alm, 'ma', split_axis=3, concat_axis=2, tiled=True)]
    unnamed x6 -> x5, local copies, waits for them, and re-layouts: 3.01 us -> 2.69 us
where the time goes in v1:
time: 98.4 us; the launch traced here: 98.1 us
  blocking collectives  56.4 us (57%)
  between operations  19.1 us (19%)
  local copies, waits for them, and re-layouts  9.32 us (9%)
  waiting for transfers between devices  8.54 us (9%)
  matrix products  3.01 us (3%)
  other arithmetic  1.79 us (2%)
    all_to_all x1, blocking collectives, loops_follow(): lax.all_to_all(jnp.stack(jnp.split(m, lax.psum(1, axis_name='ma'), axis=3...  32 us
    psum x1, blocking collectives, on_device(): channel_power = lax.psum(partial_power, ('ma', 'pol')) / modes_total  17.7 us
    all_gather x1, waiting for transfers between devices, on_device(): joined = lax.all_gather(blocks, 'pol', axis=3, tiled=True)  8.53 us
    psum x1, blocking collectives, on_device(): lax.psum((jnp.sum(mask_float * channel_power), jnp.sum(mask_float)), 'freq')  6.71 us
    split x1, local copies, waits for them, and re-layouts, loops_follow(): jnp.split(m, lax.psum(1, axis_name='ma'), axis=3)  4.66 us
    unnamed x5, local copies, waits for them, and re-layouts  2.69 us
  transfers between devices with their start and end apart: 1, of which 1 were waited for; matrix products, arithmetic and copies ran while one was open for 0% of the time, Pallas kernels for 0%

profile of v1, /device:TPU:0, one launch (start us, length us, event | category | flops | bytes accessed | tf_op | source)
XLA Modules:
  0.0 98.1 jit_solution(8006794011398437174)
XLA Ops:
  7.2 0.0 all-gather.3.cloned.1.call-start
  7.2 4.7 %fusion.5 = (bf16[2,1,128,1,512]{4,3,2,1,0:T(2,128)(2,1)S(1)}, bf16[2,1,128,1,512]{4,3,2,1,0:T(2,128)(2,1)S(1)}, bf16[2,1,128,1,512]{4,3,2,1,0:T(2,128)(2,1)S(1)}, bf16[2,1,128,1,512]{4,3,2,1,0:T(2,128)(2,1)S(1)}) fusion(bf16[2,1,128,4,512]{4,3,2,1,0:T(4,128)(2,1)} %param.5), kind=kLoop, calls=%fused_computation.21 | loop fusion | bytes 2097152 | tf_op jit(solution)/shard_map/split | solution.py:9
  11.9 0.1 copy_bitcast_fusion.2
  12.0 0.1 copy_bitcast_fusion
  12.1 0.1 pad_maximum_fusion
  12.3 32.0 %all_to_all.5 = bf16[4,2,1,128,1,512]{5,3,1,4,2,0:T(8,128)(2,1)} all-to-all(bf16[4,2,1,128,1,512]{5,3,1,4,2,0:T(8,128)(2,1)S(1)} %pad_maximum_fusion), channel_id=1, replica_groups=mesh['sky'=2,'ma'=4,'freq'=2,'pol'=2] {'ma'}, dimensions={0} | all-to-all | bytes 2097152 | tf_op jit(solution)/shard_map/all_to_all | solution.py:8
  44.3 0.0 all-gather.3.cloned.1.call-update
  45.6 8.5 %all-gather.3.cloned.1.call-done = bf16[2,1,4,256,1,512]{5,3,0,4,1,2:T(8,128)(2,1)} async-done(((bf16[2,1,4,128,1,512]{5,3,0,4,1,2:T(8,128)(2,1)}), bf16[2,1,4,256,1,512]{5,3,0,4,1,2:T(8,128)(2,1)}) %all-gather.3.cloned.1.call-update) | async-done | bytes 2097168 | tf_op jit(solution)/shard_map/all_gather | solution.py:27
  54.1 1.7 %copy.15 = bf16[2,1,4,256,1,512]{5,3,2,0,4,1:T(8,128)(2,1)S(1)} copy(bf16[2,1,4,256,1,512]{5,3,0,4,1,2:T(8,128)(2,1)} %all-gather.3.cloned.1.call-done) | data formatting | bytes 4194304 | tf_op jit(solution)/shard_map/all_gather | solution.py:27
  55.9 0.0 copy-start.1
  55.9 0.2 broadcast_select_fusion
  56.1 1.4 %copy-done.1 = bf16[1,1,2,512,1024]{4,3,2,1,0:T(8,128)(2,1)S(1)} copy-done((bf16[1,1,2,512,1024]{4,3,2,1,0:T(8,128)(2,1)S(1)}, bf16[1,1,2,512,1024]{4,3,2,1,0:T(8,128)(2,1)}, u32[]{:S(2)}) %copy-start.1) | copy-done | bytes 2097176
  57.4 0.8 fusion.3
  58.2 0.8 fusion.4
  59.0 0.8 convolution_subtract_fusion
  59.7 0.0 copy-start
  59.7 0.8 convolution_add_fusion
  60.5 0.0 copy-done
  60.5 1.1 %fusion.2 = f32[]{:T(128)} fusion(f32[1,1,512,512]{2,3,1,0:T(8,128)S(1)} %bitcast.50, f32[1,1,512,512]{2,3,1,0:T(8,128)S(1)} %bitcast.48, f32[512]{0:T(512)S(1)} %bitcast.52), kind=kLoop, calls=%fused_computation.4 | loop fusion | flops 2097151 | bytes 2099204 | tf_op jit(solution)/shard_map/reduce_sum | solution.py:43
  61.6 17.7 %psum.21 = f32[1]{0:T(128)} all-reduce(f32[1]{0:T(128)} %bitcast.19), channel_id=1, replica_groups=mesh['sky'=2,'ma'=4,'freq'=2,'pol'=2] {'ma','pol'}, use_global_device_ids=true, to_apply=%region_1.2 | all-reduce | flops 1 | bytes 8 | tf_op jit(solution)/shard_map/psum | solution.py:48
  80.5 6.7 %all-reduce = (f32[]{:T(128)}, f32[]{:T(128)}) all-reduce(f32[]{:T(128)} %bitcast.20, f32[]{:T(128)} %bitcast.21), channel_id=1, replica_groups=mesh['sky'=2,'ma'=4,'freq'=2,'pol'=2] {'freq'}, use_global_device_ids=true, to_apply=%region_2.3 | all-reduce | flops 2 | bytes 16 | tf_op jit(solution)/shard_map/psum | solution.py:49
  88.5 0.3 fusion
  88.8 1.3 %copy.16 = bf16[2,1,1,512,512]{4,3,2,1,0:T(8,128)(2,1)} copy(bf16[2,1,1,512,512]{3,4,2,1,0:T(8,128)(2,1)S(1)} %fusion) | data formatting | bytes 2097152
  (2 shorter events, 0.0 us)
Async XLA Ops:
  7.2 47.0 %all-gather.3.cloned.1.call-start = ((), (), s32[]{:S(2)}) async-start(), calls=%async_computation.1 | async-start | bytes 3145728 | tf_op jit(solution)/shard_map/all_gather | solution.py:27
  55.9 1.6 %copy-start.1 = (bf16[1,1,2,512,1024]{4,3,2,1,0:T(8,128)(2,1)S(1)}, bf16[1,1,2,512,1024]{4,3,2,1,0:T(8,128)(2,1)}, u32[]{:S(2)}) copy-start(bf16[1,1,2,512,1024]{4,3,2,1,0:T(8,128)(2,1)} %param.6) | copy-start | bytes 6291460
  59.7 0.8 copy-start
Sparse Core Ops, SparseCore 0:
  44.4 9.6 all-gather.2
